TPU v7x, 32 devices: a whole 2x2x4 slice. The times are simulated.
32 devices in a mesh: replica: 2 (over x), fsdp: 16 (over z, y, core).
Axes of the slice: x: 2, y: 2, z: 4, core: 2. Of those that a mesh axis runs over, the one named last changes fastest.
Arguments:
- tokens: bfloat16 [16384, 1152], P(('replica', 'fsdp')), may hold values from -6 to 6
- cotangent: bfloat16 [16384, 1152], P(('replica', 'fsdp')), may hold values from -6 to 6
- piece_starts: int32 [32, 1], P(('replica', 'fsdp')), may hold values from 0 to 256, as said below
- w_query: bfloat16 [1152, 1024], P('fsdp'), may hold values from -0.1875 to 0.1875
- w_key: bfloat16 [1152, 256], P('fsdp'), may hold values from -0.1875 to 0.1875
- w_value: bfloat16 [1152, 256], P('fsdp'), may hold values from -0.1875 to 0.1875
- w_out: bfloat16 [1024, 1152], P('fsdp'), may hold values from -0.1875 to 0.1875
- w_gate: bfloat16 [1152, 6912], P('fsdp'), may hold values from -0.1875 to 0.1875
- w_up: bfloat16 [1152, 6912], P('fsdp'), may hold values from -0.1875 to 0.1875
- w_down: bfloat16 [6912, 1152], P('fsdp'), may hold values from -0.078125 to 0.078125
- attn_pre_gain: bfloat16 [1152], P('fsdp'), may hold values from 0.5 to 1.5
- query_gain: bfloat16 [256], P('fsdp'), may hold values from 1 to 2.5
- key_gain: bfloat16 [256], P('fsdp'), may hold values from 0.25 to 1.75
- attn_post_gain: bfloat16 [1152], P('fsdp'), may hold values from 0.25 to 1.75
- mlp_pre_gain: bfloat16 [1152], P('fsdp'), may hold values from 0.5 to 1.5
- mlp_post_gain: bfloat16 [1152], P('fsdp'), may hold values from 0.25 to 1.75
Outputs:
- layer_out: bfloat16 [16384, 1152], P(('replica', 'fsdp'))
- input_grad: float32 [16384, 1152], P(('replica', 'fsdp'))
- grad_query: float32 [1152, 1024], P('fsdp')
- grad_key: float32 [1152, 256], P('fsdp')
- grad_value: float32 [1152, 256], P('fsdp')
- grad_out: float32 [1024, 1152], P('fsdp')
- grad_gate: float32 [1152, 6912], P('fsdp')
- grad_up: float32 [1152, 6912], P('fsdp')
- grad_down: float32 [6912, 1152], P('fsdp')
- grad_attn_pre: float32 [1152], P('fsdp')
- grad_query_gain: float32 [256], P('fsdp')
- grad_key_gain: float32 [256], P('fsdp')
- grad_attn_post: float32 [1152], P('fsdp')
- grad_mlp_pre: float32 [1152], P('fsdp')
- grad_mlp_post: float32 [1152], P('fsdp')
Inputs may be any that keep to these rules, and one draw needn't show every extreme that they name: `piece_starts`: each row holds the starts of the 1 image pieces of 256 tokens in one sequence, rising, the pieces disjoint and within the sequence's 512 tokens; the other tokens of the sequence are causal text.
All inputs are finite; a program needn't handle non-finite values.
Results may differ from a plain program's by a relative error of at most 0.018.
Values may be sent and summed in bfloat16 or wider, within the bound.
A program may use at most 320 MiB of HBM per device.

v0:
```python
import jax
import jax.numpy as jnp
from jax import lax
from jax.sharding import PartitionSpec as P

D = 1152
H = 4
HD = 256
FF = 6912
PIECE = 256
epsilon = 1e-06
rope_base = 1000000.0
masked_value = -1e30


def row_scale(values):
    return lax.rsqrt(jnp.mean(values * values, axis=-1, keepdims=True) + epsilon)


def norm_back(values, scale, gain, upstream):
    weighted = upstream * gain
    inner = jnp.mean(weighted * values, axis=-1, keepdims=True)
    grad_values = scale * weighted - values * (scale * scale * scale) * inner
    grad_gain = jnp.sum((upstream * values * scale).reshape(-1, values.shape[-1]), axis=0)
    return (grad_values, grad_gain)


def rope_tables(length, width):
    positions = jnp.arange(length, dtype=jnp.float32)
    freqs = rope_base ** (-jnp.arange(width // 2, dtype=jnp.float32) * 2.0 / width)
    angles = positions[:, None] * freqs[None, :]
    return (jnp.cos(angles), jnp.sin(angles))


def rotate(values, cosine, sine):
    half = values.shape[-1] // 2
    first = values[..., :half]
    second = values[..., half:]
    return jnp.concatenate(
        [first * cosine - second * sine, second * cosine + first * sine], axis=-1
    )


def rotate_back(upstream, cosine, sine):
    half = upstream.shape[-1] // 2
    first = upstream[..., :half]
    second = upstream[..., half:]
    return jnp.concatenate(
        [first * cosine + second * sine, second * cosine - first * sine], axis=-1
    )


def score_mask(rows, columns, starts):
    inside_rows = (rows[None, :] >= starts[:, None]) & (rows[None, :] < starts[:, None] + PIECE)
    inside_cols = (columns[None, :] >= starts[:, None]) & (
        columns[None, :] < starts[:, None] + PIECE
    )
    same = jnp.any(inside_rows[:, :, None] & inside_cols[:, None, :], axis=0)
    return (columns[None, :] <= rows[:, None]) | same


def matmul(left, right):
    return jnp.dot(left, right, preferred_element_type=jnp.float32)


def matmul_back(left, right):
    return lax.dot_general(
        left, right, (((1,), (1,)), ((), ())), preferred_element_type=jnp.float32
    )


def term_maker(left, rights):

    def term(start, count):
        parts = [
            lax.dot_general(
                left, right, (((0,), (0,)), ((), ())), preferred_element_type=jnp.float32
            )
            for right in rights
        ]
        return jnp.concatenate(parts, axis=1)

    return term


def on_device(
    tokens,
    cotangent,
    piece_starts,
    w_query,
    w_key,
    w_value,
    w_out,
    w_gate,
    w_up,
    w_down,
    attn_pre_gain,
    query_gain,
    key_gain,
    attn_post_gain,
    mlp_pre_gain,
    mlp_post_gain,
):
    length = tokens.shape[0]
    starts = piece_starts[0]
    fsdp_count = lax.axis_size("fsdp")
    attn_full = (
        lax.all_gather(w_query, "fsdp", axis=0, tiled=True),
        lax.all_gather(w_key, "fsdp", axis=0, tiled=True),
        lax.all_gather(w_value, "fsdp", axis=0, tiled=True),
        lax.all_gather(w_out, "fsdp", axis=0, tiled=True),
        lax.all_gather(attn_pre_gain, "fsdp", axis=0, tiled=True),
        lax.all_gather(query_gain, "fsdp", axis=0, tiled=True),
        lax.all_gather(key_gain, "fsdp", axis=0, tiled=True),
        lax.all_gather(attn_post_gain, "fsdp", axis=0, tiled=True),
    )
    gain_attn_pre = attn_full[4].astype(jnp.float32)
    gain_query = attn_full[5].astype(jnp.float32)
    gain_key = attn_full[6].astype(jnp.float32)
    gain_attn_post = attn_full[7].astype(jnp.float32)
    inputs = tokens.astype(jnp.float32)
    scale_attn = row_scale(inputs)
    normed_attn = (inputs * scale_attn * gain_attn_pre).astype(jnp.bfloat16)
    query_proj = matmul(normed_attn, attn_full[0]).reshape(length, H, HD)
    key_proj = matmul(normed_attn, attn_full[1])
    value_proj = matmul(normed_attn, attn_full[2])
    cosine, sine = rope_tables(length, HD)
    attn_factor = HD ** (-0.5)
    scale_query = row_scale(query_proj)
    query_low = (
        rotate(query_proj * scale_query * gain_query, cosine[:, None, :], sine[:, None, :])
        * attn_factor
    ).astype(jnp.bfloat16)
    scale_key = row_scale(key_proj)
    key_low = rotate(key_proj * scale_key * gain_key, cosine, sine).astype(jnp.bfloat16)
    value_low = value_proj.astype(jnp.bfloat16)
    count = length // length
    columns = jnp.arange(length, dtype=jnp.int32)
    block_ids = jnp.arange(count, dtype=jnp.int32)
    query_blocks = query_low.reshape(count, length, H, HD)

    def attend(item):
        index, queries = item
        rows = index * length + jnp.arange(length, dtype=jnp.int32)
        allowed = score_mask(rows, columns, starts)
        scores = jnp.einsum("thd,sd->hts", queries, key_low, preferred_element_type=jnp.float32)
        scores = jnp.where(allowed[None], scores, masked_value)
        peak = jnp.max(scores, axis=-1, keepdims=True)
        expo = jnp.exp(scores - peak)
        total = jnp.sum(expo, axis=-1, keepdims=True)
        probs_low = (expo / total).astype(jnp.bfloat16)
        mixed_part = jnp.einsum(
            "hts,sd->thd", probs_low, value_low, preferred_element_type=jnp.float32
        )
        return (mixed_part, (peak + jnp.log(total))[..., 0])

    mixed_parts, logsums = lax.map(attend, (block_ids, query_blocks))
    mixed_low = mixed_parts.reshape(length, H * HD).astype(jnp.bfloat16)
    attn_out = matmul(mixed_low, attn_full[3])
    scale_post = row_scale(attn_out)
    resid = inputs + attn_out * scale_post * gain_attn_post
    mlp_full = (
        lax.all_gather(w_gate, "fsdp", axis=0, tiled=True),
        lax.all_gather(w_up, "fsdp", axis=0, tiled=True),
        lax.all_gather(w_down, "fsdp", axis=0, tiled=True),
        lax.all_gather(mlp_pre_gain, "fsdp", axis=0, tiled=True),
        lax.all_gather(mlp_post_gain, "fsdp", axis=0, tiled=True),
    )
    gain_mlp_pre = mlp_full[3].astype(jnp.float32)
    gain_mlp_post = mlp_full[4].astype(jnp.float32)
    scale_mlp = row_scale(resid)
    normed_mlp = (resid * scale_mlp * gain_mlp_pre).astype(jnp.bfloat16)
    gate = matmul(normed_mlp, mlp_full[0])
    upper = matmul(normed_mlp, mlp_full[1])
    activated, gelu_pull = jax.vjp(lambda values: jax.nn.gelu(values, approximate=True), gate)
    hidden_low = (activated * upper).astype(jnp.bfloat16)
    mlp_out = matmul(hidden_low, mlp_full[2])
    scale_out = row_scale(mlp_out)
    layer_out = (resid + mlp_out * scale_out * gain_mlp_post).astype(jnp.bfloat16)
    upstream = cotangent.astype(jnp.float32)
    grad_mlp_out, grad_mlp_post = norm_back(mlp_out, scale_out, gain_mlp_post, upstream)
    grad_mlp_low = grad_mlp_out.astype(jnp.bfloat16)
    grad_hidden = matmul_back(grad_mlp_low, mlp_full[2])
    grad_gate_low = gelu_pull(grad_hidden * upper)[0].astype(jnp.bfloat16)
    grad_up_low = (grad_hidden * activated).astype(jnp.bfloat16)
    grad_normed_mlp = matmul_back(grad_gate_low, mlp_full[0]) + matmul_back(
        grad_up_low, mlp_full[1]
    )
    grad_resid_part, grad_mlp_pre = norm_back(resid, scale_mlp, gain_mlp_pre, grad_normed_mlp)
    grad_resid = upstream + grad_resid_part
    mlp_in_term = term_maker(normed_mlp, (grad_gate_low, grad_up_low))
    down_term = term_maker(hidden_low, (grad_mlp_low,))
    mlp_in_share = lax.psum_scatter(
        mlp_in_term(jnp.int32(0), lax.axis_size("fsdp") * (D // fsdp_count)),
        "fsdp",
        scatter_dimension=0,
        tiled=True,
    )
    down_share = lax.psum_scatter(
        down_term(jnp.int32(0), lax.axis_size("fsdp") * (FF // fsdp_count)),
        "fsdp",
        scatter_dimension=0,
        tiled=True,
    )
    grad_attn_out, grad_attn_post = norm_back(attn_out, scale_post, gain_attn_post, grad_resid)
    grad_attn_low = grad_attn_out.astype(jnp.bfloat16)
    grad_mixed_low = matmul_back(grad_attn_low, attn_full[3]).astype(jnp.bfloat16)
    grad_blocks = grad_mixed_low.reshape(count, length, H, HD)

    def attend_back(carry, item):
        key_total, value_total = carry
        index, queries, grads, logsum = item
        rows = index * length + jnp.arange(length, dtype=jnp.int32)
        allowed = score_mask(rows, columns, starts)
        scores = jnp.einsum("thd,sd->hts", queries, key_low, preferred_element_type=jnp.float32)
        scores = jnp.where(allowed[None], scores, masked_value)
        probs = jnp.exp(scores - logsum[..., None])
        probs_low = probs.astype(jnp.bfloat16)
        grad_probs = jnp.einsum("thd,sd->hts", grads, value_low, preferred_element_type=jnp.float32)
        value_total = value_total + jnp.einsum(
            "hts,thd->sd", probs_low, grads, preferred_element_type=jnp.float32
        )
        inner = jnp.sum(probs * grad_probs, axis=-1, keepdims=True)
        grad_scores = (probs * (grad_probs - inner)).astype(jnp.bfloat16)
        grad_queries = jnp.einsum(
            "hts,sd->thd", grad_scores, key_low, preferred_element_type=jnp.float32
        )
        key_total = key_total + jnp.einsum(
            "hts,thd->sd", grad_scores, queries, preferred_element_type=jnp.float32
        )
        return ((key_total, value_total), grad_queries)

    zero_rows = jnp.zeros((length, HD), jnp.float32)
    (grad_key_rot, grad_value_act), grad_query_parts = lax.scan(
        attend_back, (zero_rows, zero_rows), (block_ids, query_blocks, grad_blocks, logsums)
    )
    grad_query_act = grad_query_parts.reshape(length, H, HD)
    grad_query_normed = rotate_back(
        grad_query_act * attn_factor, cosine[:, None, :], sine[:, None, :]
    )
    grad_query_proj, grad_query_gain = norm_back(
        query_proj, scale_query, gain_query, grad_query_normed
    )
    grad_key_normed = rotate_back(grad_key_rot, cosine, sine)
    grad_key_proj, grad_key_gain = norm_back(key_proj, scale_key, gain_key, grad_key_normed)
    grad_query_low = grad_query_proj.reshape(length, H * HD).astype(jnp.bfloat16)
    grad_key_low = grad_key_proj.astype(jnp.bfloat16)
    grad_value_low = grad_value_act.astype(jnp.bfloat16)
    grad_normed_attn = (
        matmul_back(grad_query_low, attn_full[0])
        + matmul_back(grad_key_low, attn_full[1])
        + matmul_back(grad_value_low, attn_full[2])
    )
    grad_input_part, grad_attn_pre = norm_back(inputs, scale_attn, gain_attn_pre, grad_normed_attn)
    input_grad = grad_resid + grad_input_part
    attn_in_term = term_maker(normed_attn, (grad_query_low, grad_key_low, grad_value_low))
    out_term = term_maker(mixed_low, (grad_attn_low,))
    attn_in_share = lax.psum_scatter(
        attn_in_term(jnp.int32(0), lax.axis_size("fsdp") * (D // fsdp_count)),
        "fsdp",
        scatter_dimension=0,
        tiled=True,
    )
    out_share = lax.psum_scatter(
        out_term(jnp.int32(0), lax.axis_size("fsdp") * (H * HD // fsdp_count)),
        "fsdp",
        scatter_dimension=0,
        tiled=True,
    )
    gains_all = lax.psum(
        (
            grad_attn_pre,
            grad_query_gain,
            grad_key_gain,
            grad_attn_post,
            grad_mlp_pre,
            grad_mlp_post,
        ),
        ("replica", "fsdp"),
    )
    owner = lax.axis_index("fsdp")
    d_rows = D // fsdp_count
    h_rows = HD // fsdp_count
    gain_shares = (
        lax.dynamic_slice_in_dim(gains_all[0], owner * d_rows, d_rows, 0),
        lax.dynamic_slice_in_dim(gains_all[1], owner * h_rows, h_rows, 0),
        lax.dynamic_slice_in_dim(gains_all[2], owner * h_rows, h_rows, 0),
        lax.dynamic_slice_in_dim(gains_all[3], owner * d_rows, d_rows, 0),
        lax.dynamic_slice_in_dim(gains_all[4], owner * d_rows, d_rows, 0),
        lax.dynamic_slice_in_dim(gains_all[5], owner * d_rows, d_rows, 0),
    )
    results = (
        lax.psum(attn_in_share.astype(jnp.bfloat16), "replica").astype(jnp.float32),
        lax.psum(out_share.astype(jnp.bfloat16), "replica").astype(jnp.float32),
        lax.psum(mlp_in_share.astype(jnp.bfloat16), "replica").astype(jnp.float32),
        lax.psum(down_share.astype(jnp.bfloat16), "replica").astype(jnp.float32),
    )
    attn_in_full = results[0]
    mlp_in_full = results[2]
    qwidth = H * HD
    grad_query = attn_in_full[:, :qwidth]
    grad_key = attn_in_full[:, qwidth : qwidth + HD]
    grad_value = attn_in_full[:, qwidth + HD :]
    grad_gate = mlp_in_full[:, :FF]
    grad_up = mlp_in_full[:, FF:]
    return (
        layer_out,
        input_grad,
        grad_query,
        grad_key,
        grad_value,
        results[1],
        grad_gate,
        grad_up,
        results[3],
        gain_shares[0],
        gain_shares[1],
        gain_shares[2],
        gain_shares[3],
        gain_shares[4],
        gain_shares[5],
    )


def solution(mesh):
    placed = (
        P(("replica", "fsdp"), None),
        P(("replica", "fsdp"), None),
        P(("replica", "fsdp"), None),
        P("fsdp", None),
        P("fsdp", None),
        P("fsdp", None),
        P("fsdp", None),
        P("fsdp", None),
        P("fsdp", None),
        P("fsdp", None),
        P("fsdp"),
        P("fsdp"),
        P("fsdp"),
        P("fsdp"),
        P("fsdp"),
        P("fsdp"),
    )
    return jax.shard_map(
        on_device,
        mesh=mesh,
        in_specs=placed,
        out_specs=(
            P(("replica", "fsdp"), None),
            P(("replica", "fsdp"), None),
            P("fsdp", None),
            P("fsdp", None),
            P("fsdp", None),
            P("fsdp", None),
            P("fsdp", None),
            P("fsdp", None),
            P("fsdp", None),
            P("fsdp"),
            P("fsdp"),
            P("fsdp"),
            P("fsdp"),
            P("fsdp"),
            P("fsdp"),
        ),
        check_vma=False,
    )
```

profile of v0, /device:TPU:0, one launch (start us, length us, event | category | flops | bytes accessed | tf_op | source)
XLA Modules:
  0.0 1775.8 jit_solution(9544685377612976665)
XLA Ops:
  14.8 63.6 %all-reduce.8 = (bf16[1152]{0:T(1024)(128)(2,1)S(1)}, bf16[256]{0:T(256)(128)(2,1)S(1)}, bf16[256]{0:T(256)(128)(2,1)S(1)}, bf16[1152]{0:T(1024)(128)(2,1)S(1)},...) all-reduce(bf16[1152]{0:T(1024)(128)(2,1)S(1)} %dynamic-update-slic, ...), channel_id=1, replica_groups=mesh['replica'=2,'fsdp'=16] {'fsdp'}, use_global_device_ids=true, to_apply=%add | all-reduce | flops 5120 | bytes 20480
  81.0 21.2 %all_gather.41 = bf16[1152,256]{1,0:T(8,128)(2,1)S(1)} all-gather(bf16[72,256]{1,0:T(8,128)(2,1)S(1)} %copy-done.69), channel_id=1, replica_groups=mesh['replica'=2,'fsdp'=16] {'fsdp'}, dimensions={0}, use_global_device_ids=true | all-gather | bytes 626688 | tf_op jit(solution)/shard_map/all_gather | solution.py:109
  108.0 21.2 %all_gather.40 = bf16[1152,256]{1,0:T(8,128)(2,1)S(1)} all-gather(bf16[72,256]{1,0:T(8,128)(2,1)S(1)} %copy-done.70), channel_id=1, replica_groups=mesh['replica'=2,'fsdp'=16] {'fsdp'}, dimensions={0}, use_global_device_ids=true | all-gather | bytes 626688 | tf_op jit(solution)/shard_map/all_gather | solution.py:110
  130.5 3.2 fusion.79
  136.2 2.9 multiply_reduce_fusion.7
  148.0 3.7 multiply_reduce_fusion.6
  153.9 71.6 %all-gather.10.cloned.1.call-done = bf16[1152,6912]{1,0:T(8,128)(2,1)} async-done(((bf16[72,6912]{1,0:T(8,128)(2,1)}), bf16[1152,6912]{1,0:T(8,128)(2,1)}) %all-gather.10.cloned.1.call-update) | async-done | bytes 15925264 | tf_op jit(solution)/shard_map/all_gather | solution.py:163
  225.6 16.0 fusion.86
  241.5 105.8 %all-gather.12.cloned.1.call-done = bf16[1152,6912]{1,0:T(8,128)(2,1)} async-done(((bf16[72,6912]{1,0:T(8,128)(2,1)}), bf16[1152,6912]{1,0:T(8,128)(2,1)}) %all-gather.12.cloned.1.call-update) | async-done | bytes 15925264 | tf_op jit(solution)/shard_map/all_gather | solution.py:164
  347.3 21.5 %multiply_convert_fusion.1 = (bf16[512,6912]{1,0:T(8,128)(2,1)}, f32[512,6912]{1,0:T(8,128)}) fusion(f32[512,6912]{1,0:T(8,128)} %fusion.86, bf16[512,1152]{1,0:T(8,128)(2,1)S(1)} %multiply_convert_fusion.2, bf16[1152,6912]{1,0:T(8,128)(2,1)} %all-gather.12.cloned.1.call-done), kind=kOutput, calls=%fused_computation.11 | convolution fusion | flops 8189116416 | bytes 52494336 | tf_op jit(solution)/shard_map/dot_general | solution.py:63
  368.8 100.3 %all-gather.14.cloned.1.call-done = bf16[6912,1152]{1,0:T(8,128)(2,1)} async-done(((bf16[432,1152]{1,0:T(8,128)(2,1)}), bf16[6912,1152]{1,0:T(8,128)(2,1)}) %all-gather.14.cloned.1.call-update) | async-done | bytes 15925264 | tf_op jit(solution)/shard_map/all_gather | solution.py:165
  469.1 14.5 multiply_reduce_fusion.4
  487.3 28.6 %multiply_convert_fusion = (bf16[512,6912]{1,0:T(8,128)(2,1)}, bf16[512,6912]{1,0:T(8,128)(2,1)}) fusion(f32[512,6912]{1,0:T(8,128)} %fusion.86, f32[512,6912]{1,0:T(8,128)} %get-tuple-element.216, bf16[6912,1152]{1,0:T(8,128)(2,1)} %all-gather.14.cloned.1.call-done, bf16[512,1152]{1,0:T(8,128)(2,1)S(1)} %copy-done.26, f32[512,1152]{1,0:T(8,128)} %copy-done.33, ...), kind=kOutput, calls=%fused_computation.10 | convolution fusion | flops 8242790400 | bytes 61942272 | tf_op jit(solution)/shard_map/dot_general | solution.py:67
  515.9 15.7 fusion.87
  531.7 16.0 multiply_reduce_fusion
  552.0 3.7 fusion.89
  587.4 3.9 fusion.77
  591.3 5.7 pad_maximum_fusion.1
  597.0 8.1 copy.151
  605.8 18.6 %fusion.69 = f32[6912,1152]{1,0:T(8,128)} fusion(bf16[512,6912]{1,0:T(8,128)(2,1)} %get-tuple-element.215, bf16[512,1152]{1,0:T(8,128)(2,1)} %param.17, f32[512,1152]{1,0:T(8,128)} %copy-done.33, f32[512]{0:T(512)S(1)} %copy-done.101, f32[512]{0:T(512)S(1)} %copy-done.100, f32[1152]{0:T(1024)S(1)} %copy-done.81, f32[512]{0:T(512)S(1)} %copy-done.95), kind=kOutput, calls=%fused_computation.148 | convolution fusion | flops 8157855744 | bytes 42478080 | tf_op jit(solution)/shard_map/dot_general | solution.py:76
  624.6 19.4 %fusion.91 = f32[1152,6912]{1,0:T(8,128)} fusion(bf16[512,1152]{1,0:T(8,128)(2,1)} %copy-done.11, bf16[512,6912]{1,0:T(8,128)(2,1)} %get-tuple-element.176), kind=kOutput, calls=%fused_computation.162 | convolution fusion | flops 8153726976 | bytes 40108032 | tf_op jit(solution)/shard_map/dot_general | solution.py:76
  644.0 17.8 %fusion.90 = f32[1152,6912]{1,0:T(8,128)} fusion(bf16[512,1152]{1,0:T(8,128)(2,1)S(1)} %copy-done.12, bf16[512,6912]{1,0:T(8,128)(2,1)} %get-tuple-element.177), kind=kOutput, calls=%fused_computation.161 | convolution fusion | flops 8153726976 | bytes 40108032 | tf_op jit(solution)/shard_map/dot_general | solution.py:76
  661.8 44.3 %pad_maximum_fusion = f32[1152,13824]{1,0:T(8,128)} fusion(f32[1152,6912]{1,0:T(8,128)} %fusion.91, f32[1152,6912]{1,0:T(8,128)} %fusion.90), kind=kLoop, calls=%fused_computation | loop fusion | flops 15925248 | bytes 127401984 | tf_op jit(solution)/shard_map/concatenate | solution.py:81
  707.8 15.4 reduce-scatter.13.cloned.1.call-done
  725.2 322.3 %reduce-scatter.11.cloned.1.call-done = f32[432,1152]{1,0:T(8,128)} async-done(((f32[6912,1152]{1,0:T(8,128)}), f32[432,1152]{1,0:T(8,128)}) %reduce-scatter.11.cloned.1.call-update) | async-done | bytes 1990672 | tf_op jit(solution)/shard_map/reduce_scatter | solution.py:199
  1047.5 2.6 convert_element_type.146
  1050.1 608.0 %reduce-scatter.15.cloned.1.call-done = f32[72,13824]{1,0:T(8,128)} async-done(((f32[1152,13824]{1,0:T(8,128)}), f32[72,13824]{1,0:T(8,128)}) %reduce-scatter.15.cloned.1.call-update) | async-done | bytes 3981328
  1658.1 3.6 convert_element_type.144
  1671.8 2.9 fusion.28
  1674.7 41.3 %all-reduce.7 = (f32[1152]{0:T(1024)}, f32[256]{0:T(256)}, f32[256]{0:T(256)}, f32[1152]{0:T(1024)}, f32[1152]{0:T(1024)}, /*index=5*/f32[1152]{0:T(1024)}) all-reduce(f32[1152]{0:T(1024)} %get-tuple-element.153, f32[256]{0:T(256)} %fusion.35, f32[256]{0:T(256)} %get-tuple-element.155, ...), channel_id=1, replica_groups=mesh['replica'=2,'fsdp'=16] {'replica','fsdp'}, use_global_device_ids=true, to_apply=%region_24.25 | all-reduce | flops 5120 | bytes 40960 | tf_op jit(solution)/shard_map/psum | solution.py:270
  1724.3 3.7 fusion.25
  1728.0 28.5 %all-reduce.12.cloned.1.call-done = (bf16[72,1536]{0,1:T(8,128)(2,1)}, bf16[72,13824]{1,0:T(8,128)(2,1)}, bf16[64,1152]{1,0:T(8,128)(2,1)}, bf16[432,1152]{1,0:T(8,128)(2,1)}) async-done(((bf16[72,1536]{0,1:T(8,128)(2,1)}, bf16[72,13824]{1,0:T(8,128)(2,1)}, bf16[64,1152]{1,0:T(8,128)(2,1)}, bf16[432,1152]{1,0:T(8,128)(2,1)}), (bf16[72,1536]{0,1:T(8,128)(2,1)}, bf16[72,13824]{1,0:T(8,128)(2,1)}, ...) | async-done | bytes 3354640 | tf_op jit(solution)/shard_map/psum | solution.py:293
  (346 shorter events, 102.7 us)
Async XLA Ops:
  7.3 72.9 %copy-start.9 = (bf16[512,1152]{1,0:T(8,128)(2,1)S(1)}, bf16[512,1152]{1,0:T(8,128)(2,1)}, u32[]{:S(2)}) copy-start(bf16[512,1152]{1,0:T(8,128)(2,1)} %param.16) | copy-start | bytes 3538948
  7.3 73.8 %copy-start.69 = (bf16[72,256]{1,0:T(8,128)(2,1)S(1)}, bf16[72,256]{1,0:T(8,128)(2,1)}, u32[]{:S(2)}) copy-start(bf16[72,256]{1,0:T(8,128)(2,1)} %param.20) | copy-start | bytes 110596
  7.3 123.2 %all-gather.6.cloned.1.call-start = ((), (), s32[]{:S(2)}) async-start(), calls=%async_computation.4 | async-start | bytes 2506752 | tf_op jit(solution)/shard_map/all_gather | solution.py:108
  8.0 140.0 %all-gather.8.cloned.1.call-start = ((), (), s32[]{:S(2)}) async-start(), calls=%async_computation.5 | async-start | bytes 2506752 | tf_op jit(solution)/shard_map/all_gather | solution.py:111
  8.8 216.8 %all-gather.10.cloned.1.call-start = ((), (), s32[]{:S(2)}) async-start(), calls=%async_computation.6 | async-start | bytes 16920576 | tf_op jit(solution)/shard_map/all_gather | solution.py:163
  9.5 337.8 %all-gather.12.cloned.1.call-start = ((), (), s32[]{:S(2)}) async-start(), calls=%async_computation.7 | async-start | bytes 16920576 | tf_op jit(solution)/shard_map/all_gather | solution.py:164
  10.1 459.0 %all-gather.14.cloned.1.call-start = ((), (), s32[]{:S(2)}) async-start(), calls=%async_computation.8 | async-start | bytes 16920576 | tf_op jit(solution)/shard_map/all_gather | solution.py:165
  10.7 695.5 %reduce-scatter.9.cloned.1.call-start = ((), (), s32[]{:S(2)}) async-start(), calls=%async_computation.9 | async-start | bytes 5013504 | tf_op jit(solution)/shard_map/reduce_scatter | solution.py:264
  78.3 25.2 %copy-start.89 = (f32[256]{0:T(256)}, f32[256]{0:T(256)S(1)}, u32[]{:S(2)}) copy-start(f32[256]{0:T(256)S(1)} %convert_element_type.116) | copy-start | bytes 3076
  78.9 51.5 %copy-start.64 = (f32[1152]{0:T(1024)}, f32[1152]{0:T(1024)S(1)}, u32[]{:S(2)}) copy-start(f32[1152]{0:T(1024)S(1)} %convert_element_type.113) | copy-start | bytes 13828
  78.9 73.4 %copy-start.62 = (f32[1152]{0:T(1024)}, f32[1152]{0:T(1024)S(1)}, u32[]{:S(2)}) copy-start(f32[1152]{0:T(1024)S(1)} %convert_element_type.123) | copy-start | bytes 13828
  80.1 24.1 %copy-start.98 = (f32[128]{0:T(128)}, f32[128]{0:T(128)S(1)}, u32[]{:S(2)}) copy-start(f32[128]{0:T(128)S(1)} %multiply_power_fusion) | copy-start | bytes 1540
  81.0 48.2 %copy-start.83 = (f32[512]{0:T(512)}, f32[512]{0:T(512)S(1)}, u32[]{:S(2)}) copy-start(f32[512]{0:T(512)S(1)} %get-tuple-element.196) | copy-start | bytes 6148
  108.0 37.3 %copy-start.29 = (pred[512,512]{0,1:T(8,128)(4,1)}, pred[512,512]{0,1:T(8,128)(4,1)S(1)}, u32[]{:S(2)}) copy-start(pred[512,512]{0,1:T(8,128)(4,1)S(1)} %fusion.52) | copy-start | bytes 786436
  153.6 87.9 %copy-start.86 = (f32[512]{0:T(512)}, f32[512]{0:T(512)S(1)}, u32[]{:S(2)}) copy-start(f32[512]{0:T(512)S(1)} %get-tuple-element.202) | copy-start | bytes 6148
  153.9 193.4 %copy-start.11 = (bf16[512,1152]{1,0:T(8,128)(2,1)}, bf16[512,1152]{1,0:T(8,128)(2,1)S(1)}, u32[]{:S(2)}) copy-start(bf16[512,1152]{1,0:T(8,128)(2,1)S(1)} %multiply_convert_fusion.2) | copy-start | bytes 3538948
  469.1 15.1 copy-start.26
  469.1 15.1 copy-start.80
  515.9 15.7 copy-start.23
  515.9 15.7 copy-start.87
  531.7 16.0 copy-start.6
  531.7 16.0 copy-start.63
  531.7 16.0 copy-start.72
  531.7 16.0 copy-start.97
  555.7 167.5 %reduce-scatter.13.cloned.1.call-start = ((), (), s32[]{:S(2)}) async-start(), calls=%async_computation.11 | async-start | bytes 7520256
  605.2 442.3 %reduce-scatter.11.cloned.1.call-start = ((), (), s32[]{:S(2)}) async-start(), calls=%async_computation.10 | async-start | bytes 33841152 | tf_op jit(solution)/shard_map/reduce_scatter | solution.py:199
  624.5 1033.6 %reduce-scatter.15.cloned.1.call-start = ((), (), s32[]{:S(2)}) async-start(), calls=%async_computation.12 | async-start | bytes 67682304
  624.6 19.4 %copy-start.12 = (bf16[512,1152]{1,0:T(8,128)(2,1)S(1)}, bf16[512,1152]{1,0:T(8,128)(2,1)}, u32[]{:S(2)}) copy-start(bf16[512,1152]{1,0:T(8,128)(2,1)} %copy-done.11) | copy-start | bytes 3538948
  706.1 1050.4 %all-reduce.12.cloned.1.call-start = ((), (), s32[]{:S(2)}) async-start(), calls=%async_computation.13 | async-start | bytes 7053312 | tf_op jit(solution)/shard_map/psum | solution.py:293
  1671.8 52.5 %copy-start.8 = (f32[512,1152]{1,0:T(8,128)S(1)}, f32[512,1152]{1,0:T(8,128)}, u32[]{:S(2)}) copy-start(f32[512,1152]{1,0:T(8,128)} %copy-done.7) | copy-start | bytes 7077892
  1756.5 8.6 copy-start.53
  1759.1 7.4 copy-start.22
  (88 other events, 202.6 us)
Sparse Core Ops, SparseCore 0:
  10.4 45.1 all-gather.5
  57.9 43.0 all-gather.7
  103.2 122.3 all-gather.9
  227.6 119.6 all-gather.11
  349.3 119.6 all-gather.13
  555.8 73.7 reduce-scatter.8
  634.1 89.0 reduce-scatter.12
  727.5 319.9 reduce-scatter.10
  1051.7 606.2 reduce-scatter.14
  1661.8 94.5 all-reduce.11
where the time goes:
time: 1780 us
  waiting for transfers between devices  1260 us (71%)
  matrix products  199 us (11%)
  blocking collectives  147 us (8%)
  other arithmetic  91.6 us (5%)
  local copies, waits for them, and re-layouts  64.5 us (4%)
    unnamed x12, waiting for transfers between devices  627 us
    reduce_scatter x1, waiting for transfers between devices, on_device(): lax.psum_scatter(down_term(jnp.int32(0), lax.axis_size('fsdp') * (FF // f...  322 us
    all_gather x1, waiting for transfers between devices, on_device(): lax.all_gather(w_up, 'fsdp', axis=0, tiled=True)  106 us
    all_gather x1, waiting for transfers between devices, on_device(): lax.all_gather(w_down, 'fsdp', axis=0, tiled=True)  100 us
    all_gather x1, waiting for transfers between devices, on_device(): lax.all_gather(w_gate, 'fsdp', axis=0, tiled=True)  71.6 us
    dot_general x7, matrix products, matmul_back(): lax.dot_general(left, right, (((1,), (1,)), ((), ())), preferred_element_...  66.8 us
    dot_general x7, matrix products, term(): lax.dot_general(left, right, (((0,), (0,)), ((), ())), preferred_element_...  64.7 us
    unnamed x1, blocking collectives  63.6 us
  transfers between devices with their start and end apart: 10, of which 7 were waited for; matrix products, arithmetic and copies ran while one was open for 13% of the time, Pallas kernels for 0%

commit v1 on v0

--- a/solution.py
+++ b/solution.py
@@ -268,15 +268,18 @@
         tiled=True,
     )
     gains_all = lax.psum(
-        (
-            grad_attn_pre,
-            grad_query_gain,
-            grad_key_gain,
-            grad_attn_post,
-            grad_mlp_pre,
-            grad_mlp_post,
+        lax.psum(
+            (
+                grad_attn_pre,
+                grad_query_gain,
+                grad_key_gain,
+                grad_attn_post,
+                grad_mlp_pre,
+                grad_mlp_post,
+            ),
+            "fsdp",
         ),
-        ("replica", "fsdp"),
+        "replica",
     )
     owner = lax.axis_index("fsdp")
     d_rows = D // fsdp_count

time: 1780 us -> 1780 us (level)
  blocking collectives: 147 us -> 177 us
  waiting for transfers between devices: 1260 us -> 1230 us
    psum x1, waiting for transfers between devices: 28.5 us -> 0.01 us  [on_device(): lax.psum(attn_in_share.astype(jnp.bfloat16), 'replica').astype(jnp.float32)]
    psum x1, blocking collectives: 41.3 us -> 60.3 us  [on_device(): lax.psum((grad_attn_pre, grad_query_gain, grad_key_gain, grad_attn_post,...]
  transfers between devices with their start and end apart: 10 -> 10, of which waited for: 7 -> 6; matrix products, arithmetic and copies ran while one was open for 13% -> 13% of each run, Pallas kernels for 0% -> 0%
where the time goes in v1:
time: 1780 us
  waiting for transfers between devices  1230 us (69%)
  matrix products  199 us (11%)
  blocking collectives  177 us (10%)
  other arithmetic  90.3 us (5%)
  local copies, waits for them, and re-layouts  63.8 us (4%)
    unnamed x12, waiting for transfers between devices  628 us
    reduce_scatter x1, waiting for transfers between devices, on_device(): lax.psum_scatter(down_term(jnp.int32(0), lax.axis_size('fsdp') * (FF // f...  322 us
    all_gather x1, waiting for transfers between devices, on_device(): lax.all_gather(w_up, 'fsdp', axis=0, tiled=True)  106 us
    all_gather x1, waiting for transfers between devices, on_device(): lax.all_gather(w_down, 'fsdp', axis=0, tiled=True)  100 us
    all_gather x1, waiting for transfers between devices, on_device(): lax.all_gather(w_gate, 'fsdp', axis=0, tiled=True)  71.7 us
    dot_general x7, matrix products, matmul_back(): lax.dot_general(left, right, (((1,), (1,)), ((), ())), preferred_element_...  66.8 us
    dot_general x7, matrix products, term(): lax.dot_general(left, right, (((0,), (0,)), ((), ())), preferred_element_...  64.6 us
    unnamed x1, blocking collectives  63.6 us
  transfers between devices with their start and end apart: 10, of which 6 were waited for; matrix products, arithmetic and copies ran while one was open for 13% of the time, Pallas kernels for 0%

profile of v1, /device:TPU:0, one launch (start us, length us, event | category | flops | bytes accessed | tf_op | source)
XLA Modules:
  0.0 1775.8 jit_solution(15106737263367518877)
XLA Ops:
  14.8 63.6 %all-reduce.9 = (bf16[1152]{0:T(1024)(128)(2,1)S(1)}, bf16[256]{0:T(256)(128)(2,1)S(1)}, bf16[256]{0:T(256)(128)(2,1)S(1)}, bf16[1152]{0:T(1024)(128)(2,1)S(1)},...) all-reduce(bf16[1152]{0:T(1024)(128)(2,1)S(1)} %dynamic-update-slic, ...), channel_id=1, replica_groups=mesh['replica'=2,'fsdp'=16] {'fsdp'}, use_global_device_ids=true, to_apply=%add | all-reduce | flops 5120 | bytes 20480
  81.0 21.2 %all_gather.41 = bf16[1152,256]{1,0:T(8,128)(2,1)S(1)} all-gather(bf16[72,256]{1,0:T(8,128)(2,1)S(1)} %copy-done.69), channel_id=1, replica_groups=mesh['replica'=2,'fsdp'=16] {'fsdp'}, dimensions={0}, use_global_device_ids=true | all-gather | bytes 626688 | tf_op jit(solution)/shard_map/all_gather | solution.py:109
  107.9 21.2 %all_gather.40 = bf16[1152,256]{1,0:T(8,128)(2,1)S(1)} all-gather(bf16[72,256]{1,0:T(8,128)(2,1)S(1)} %copy-done.70), channel_id=1, replica_groups=mesh['replica'=2,'fsdp'=16] {'fsdp'}, dimensions={0}, use_global_device_ids=true | all-gather | bytes 626688 | tf_op jit(solution)/shard_map/all_gather | solution.py:110
  130.4 3.2 fusion.79
  136.2 2.9 multiply_reduce_fusion.7
  147.9 3.7 multiply_reduce_fusion.6
  153.9 71.7 %all-gather.10.cloned.1.call-done = bf16[1152,6912]{1,0:T(8,128)(2,1)} async-done(((bf16[72,6912]{1,0:T(8,128)(2,1)}), bf16[1152,6912]{1,0:T(8,128)(2,1)}) %all-gather.10.cloned.1.call-update) | async-done | bytes 15925264 | tf_op jit(solution)/shard_map/all_gather | solution.py:163
  225.6 15.8 fusion.86
  241.4 106.0 %all-gather.12.cloned.1.call-done = bf16[1152,6912]{1,0:T(8,128)(2,1)} async-done(((bf16[72,6912]{1,0:T(8,128)(2,1)}), bf16[1152,6912]{1,0:T(8,128)(2,1)}) %all-gather.12.cloned.1.call-update) | async-done | bytes 15925264 | tf_op jit(solution)/shard_map/all_gather | solution.py:164
  347.3 21.5 %multiply_convert_fusion.1 = (bf16[512,6912]{1,0:T(8,128)(2,1)}, f32[512,6912]{1,0:T(8,128)}) fusion(f32[512,6912]{1,0:T(8,128)} %fusion.86, bf16[512,1152]{1,0:T(8,128)(2,1)S(1)} %multiply_convert_fusion.2, bf16[1152,6912]{1,0:T(8,128)(2,1)} %all-gather.12.cloned.1.call-done), kind=kOutput, calls=%fused_computation.11 | convolution fusion | flops 8189116416 | bytes 52494336 | tf_op jit(solution)/shard_map/dot_general | solution.py:63
  368.8 100.3 %all-gather.14.cloned.1.call-done = bf16[6912,1152]{1,0:T(8,128)(2,1)} async-done(((bf16[432,1152]{1,0:T(8,128)(2,1)}), bf16[6912,1152]{1,0:T(8,128)(2,1)}) %all-gather.14.cloned.1.call-update) | async-done | bytes 15925264 | tf_op jit(solution)/shard_map/all_gather | solution.py:165
  469.1 14.5 multiply_reduce_fusion.4
  487.4 28.6 %multiply_convert_fusion = (bf16[512,6912]{1,0:T(8,128)(2,1)}, bf16[512,6912]{1,0:T(8,128)(2,1)}) fusion(f32[512,6912]{1,0:T(8,128)} %fusion.86, f32[512,6912]{1,0:T(8,128)} %get-tuple-element.222, bf16[6912,1152]{1,0:T(8,128)(2,1)} %all-gather.14.cloned.1.call-done, bf16[512,1152]{1,0:T(8,128)(2,1)S(1)} %copy-done.26, f32[512,1152]{1,0:T(8,128)} %copy-done.33, ...), kind=kOutput, calls=%fused_computation.10 | convolution fusion | flops 8242790400 | bytes 61942272 | tf_op jit(solution)/shard_map/dot_general | solution.py:67
  516.0 15.7 fusion.87
  531.7 16.0 multiply_reduce_fusion
  552.0 3.7 fusion.89
  587.4 3.9 fusion.77
  591.3 5.7 pad_maximum_fusion.1
  597.0 8.1 copy.151
  605.9 18.6 %fusion.69 = f32[6912,1152]{1,0:T(8,128)} fusion(bf16[512,6912]{1,0:T(8,128)(2,1)} %get-tuple-element.221, bf16[512,1152]{1,0:T(8,128)(2,1)} %param.17, f32[512,1152]{1,0:T(8,128)} %copy-done.33, f32[512]{0:T(512)S(1)} %copy-done.101, f32[512]{0:T(512)S(1)} %copy-done.100, f32[1152]{0:T(1024)S(1)} %copy-done.81, f32[512]{0:T(512)S(1)} %copy-done.95), kind=kOutput, calls=%fused_computation.148 | convolution fusion | flops 8157855744 | bytes 42478080 | tf_op jit(solution)/shard_map/dot_general | solution.py:76
  624.6 19.3 %fusion.91 = f32[1152,6912]{1,0:T(8,128)} fusion(bf16[512,1152]{1,0:T(8,128)(2,1)} %copy-done.11, bf16[512,6912]{1,0:T(8,128)(2,1)} %get-tuple-element.182), kind=kOutput, calls=%fused_computation.162 | convolution fusion | flops 8153726976 | bytes 40108032 | tf_op jit(solution)/shard_map/dot_general | solution.py:76
  643.9 17.9 %fusion.90 = f32[1152,6912]{1,0:T(8,128)} fusion(bf16[512,1152]{1,0:T(8,128)(2,1)S(1)} %copy-done.12, bf16[512,6912]{1,0:T(8,128)(2,1)} %get-tuple-element.183), kind=kOutput, calls=%fused_computation.161 | convolution fusion | flops 8153726976 | bytes 40108032 | tf_op jit(solution)/shard_map/dot_general | solution.py:76
  661.8 42.9 %pad_maximum_fusion = f32[1152,13824]{1,0:T(8,128)} fusion(f32[1152,6912]{1,0:T(8,128)} %fusion.91, f32[1152,6912]{1,0:T(8,128)} %fusion.90), kind=kLoop, calls=%fused_computation | loop fusion | flops 15925248 | bytes 127401984 | tf_op jit(solution)/shard_map/concatenate | solution.py:81
  706.5 16.8 reduce-scatter.13.cloned.1.call-done
  725.2 321.9 %reduce-scatter.11.cloned.1.call-done = f32[432,1152]{1,0:T(8,128)} async-done(((f32[6912,1152]{1,0:T(8,128)}), f32[432,1152]{1,0:T(8,128)}) %reduce-scatter.11.cloned.1.call-update) | async-done | bytes 1990672 | tf_op jit(solution)/shard_map/reduce_scatter | solution.py:199
  1047.1 2.6 convert_element_type.146
  1049.7 608.0 %reduce-scatter.15.cloned.1.call-done = f32[72,13824]{1,0:T(8,128)} async-done(((f32[1152,13824]{1,0:T(8,128)}), f32[72,13824]{1,0:T(8,128)}) %reduce-scatter.15.cloned.1.call-update) | async-done | bytes 3981328
  1657.8 3.6 convert_element_type.144
  1671.5 2.9 fusion.28
  1674.4 60.3 %all-reduce.7 = (f32[1152]{0:T(1024)}, f32[256]{0:T(256)}, f32[256]{0:T(256)}, f32[1152]{0:T(1024)}, f32[1152]{0:T(1024)}, /*index=5*/f32[1152]{0:T(1024)}) all-reduce(f32[1152]{0:T(1024)} %get-tuple-element.153, f32[256]{0:T(256)} %fusion.35, f32[256]{0:T(256)} %get-tuple-element.155, ...), channel_id=1, replica_groups=mesh['replica'=2,'fsdp'=16] {'fsdp'}, use_global_device_ids=true, to_apply=%region_24.25 | all-reduce | flops 5120 | bytes 40960 | tf_op jit(solution)/shard_map/psum | solution.py:271
  1734.7 10.5 all-reduce.8
  1752.8 3.7 fusion.25
  (347 shorter events, 102.1 us)
Async XLA Ops:
  7.3 72.9 %copy-start.9 = (bf16[512,1152]{1,0:T(8,128)(2,1)S(1)}, bf16[512,1152]{1,0:T(8,128)(2,1)}, u32[]{:S(2)}) copy-start(bf16[512,1152]{1,0:T(8,128)(2,1)} %param.16) | copy-start | bytes 3538948
  7.3 73.8 %copy-start.69 = (bf16[72,256]{1,0:T(8,128)(2,1)S(1)}, bf16[72,256]{1,0:T(8,128)(2,1)}, u32[]{:S(2)}) copy-start(bf16[72,256]{1,0:T(8,128)(2,1)} %param.20) | copy-start | bytes 110596
  7.3 123.1 %all-gather.6.cloned.1.call-start = ((), (), s32[]{:S(2)}) async-start(), calls=%async_computation.4 | async-start | bytes 2506752 | tf_op jit(solution)/shard_map/all_gather | solution.py:108
  8.0 139.9 %all-gather.8.cloned.1.call-start = ((), (), s32[]{:S(2)}) async-start(), calls=%async_computation.5 | async-start | bytes 2506752 | tf_op jit(solution)/shard_map/all_gather | solution.py:111
  8.8 216.8 %all-gather.10.cloned.1.call-start = ((), (), s32[]{:S(2)}) async-start(), calls=%async_computation.6 | async-start | bytes 16920576 | tf_op jit(solution)/shard_map/all_gather | solution.py:163
  9.5 337.8 %all-gather.12.cloned.1.call-start = ((), (), s32[]{:S(2)}) async-start(), calls=%async_computation.7 | async-start | bytes 16920576 | tf_op jit(solution)/shard_map/all_gather | solution.py:164
  10.1 459.0 %all-gather.14.cloned.1.call-start = ((), (), s32[]{:S(2)}) async-start(), calls=%async_computation.8 | async-start | bytes 16920576 | tf_op jit(solution)/shard_map/all_gather | solution.py:165
  10.7 694.1 %reduce-scatter.9.cloned.1.call-start = ((), (), s32[]{:S(2)}) async-start(), calls=%async_computation.9 | async-start | bytes 5013504 | tf_op jit(solution)/shard_map/reduce_scatter | solution.py:264
  78.3 25.1 %copy-start.89 = (f32[256]{0:T(256)}, f32[256]{0:T(256)S(1)}, u32[]{:S(2)}) copy-start(f32[256]{0:T(256)S(1)} %convert_element_type.116) | copy-start | bytes 3076
  78.9 51.4 %copy-start.64 = (f32[1152]{0:T(1024)}, f32[1152]{0:T(1024)S(1)}, u32[]{:S(2)}) copy-start(f32[1152]{0:T(1024)S(1)} %convert_element_type.113) | copy-start | bytes 13828
  79.0 73.3 %copy-start.62 = (f32[1152]{0:T(1024)}, f32[1152]{0:T(1024)S(1)}, u32[]{:S(2)}) copy-start(f32[1152]{0:T(1024)S(1)} %convert_element_type.123) | copy-start | bytes 13828
  80.2 24.0 %copy-start.98 = (f32[128]{0:T(128)}, f32[128]{0:T(128)S(1)}, u32[]{:S(2)}) copy-start(f32[128]{0:T(128)S(1)} %multiply_power_fusion) | copy-start | bytes 1540
  81.0 48.1 %copy-start.83 = (f32[512]{0:T(512)}, f32[512]{0:T(512)S(1)}, u32[]{:S(2)}) copy-start(f32[512]{0:T(512)S(1)} %get-tuple-element.202) | copy-start | bytes 6148
  107.9 37.3 %copy-start.29 = (pred[512,512]{0,1:T(8,128)(4,1)}, pred[512,512]{0,1:T(8,128)(4,1)S(1)}, u32[]{:S(2)}) copy-start(pred[512,512]{0,1:T(8,128)(4,1)S(1)} %fusion.52) | copy-start | bytes 786436
  153.6 87.8 %copy-start.86 = (f32[512]{0:T(512)}, f32[512]{0:T(512)S(1)}, u32[]{:S(2)}) copy-start(f32[512]{0:T(512)S(1)} %get-tuple-element.208) | copy-start | bytes 6148
  153.9 193.4 %copy-start.11 = (bf16[512,1152]{1,0:T(8,128)(2,1)}, bf16[512,1152]{1,0:T(8,128)(2,1)S(1)}, u32[]{:S(2)}) copy-start(bf16[512,1152]{1,0:T(8,128)(2,1)S(1)} %multiply_convert_fusion.2) | copy-start | bytes 3538948
  469.1 15.1 copy-start.26
  469.1 15.1 copy-start.80
  516.0 15.7 copy-start.23
  516.0 15.7 copy-start.87
  531.7 16.0 copy-start.6
  531.7 16.0 copy-start.63
  531.7 16.0 copy-start.72
  531.7 16.0 copy-start.97
  555.7 167.5 %reduce-scatter.13.cloned.1.call-start = ((), (), s32[]{:S(2)}) async-start(), calls=%async_computation.11 | async-start | bytes 7520256
  605.2 442.0 %reduce-scatter.11.cloned.1.call-start = ((), (), s32[]{:S(2)}) async-start(), calls=%async_computation.10 | async-start | bytes 33841152 | tf_op jit(solution)/shard_map/reduce_scatter | solution.py:199
  624.5 1033.3 %reduce-scatter.15.cloned.1.call-start = ((), (), s32[]{:S(2)}) async-start(), calls=%async_computation.12 | async-start | bytes 67682304
  624.6 19.3 %copy-start.12 = (bf16[512,1152]{1,0:T(8,128)(2,1)S(1)}, bf16[512,1152]{1,0:T(8,128)(2,1)}, u32[]{:S(2)}) copy-start(bf16[512,1152]{1,0:T(8,128)(2,1)} %copy-done.11) | copy-start | bytes 3538948
  704.7 1051.8 %all-reduce.13.cloned.1.call-start = ((), (), s32[]{:S(2)}) async-start(), calls=%async_computation.13 | async-start | bytes 7053312 | tf_op jit(solution)/shard_map/psum | solution.py:296
  1671.5 81.3 %copy-start.8 = (f32[512,1152]{1,0:T(8,128)S(1)}, f32[512,1152]{1,0:T(8,128)}, u32[]{:S(2)}) copy-start(f32[512,1152]{1,0:T(8,128)} %copy-done.7) | copy-start | bytes 7077892
  1756.5 8.6 copy-start.53
  1759.1 7.4 copy-start.22
  (88 other events, 202.6 us)
Sparse Core Ops, SparseCore 0:
  10.4 45.1 all-gather.5
  57.9 43.0 all-gather.7
  103.2 122.3 all-gather.9
  227.6 119.6 all-gather.11
  349.4 119.6 all-gather.13
  555.9 73.6 reduce-scatter.8
  634.1 89.1 reduce-scatter.12
  727.5 319.5 reduce-scatter.10
  1051.4 606.3 reduce-scatter.14
  1661.5 94.6 all-reduce.12
